TPU v7x, 512 devices: a whole 4x4x16 slice. The times are simulated.
512 devices in a mesh: grp: 4 (over x), chan: 128 (over y, z, core).
Axes of the slice: x: 4, y: 4, z: 16, core: 2. Of those that a mesh axis runs over, the one named last changes fastest.
Arguments:
- visibilities: float32 [4, 2, 128, 16, 2, 2048], P('grp', None, 'chan'), may hold values from -12 to 12
- model: bfloat16 [4, 2, 8, 128, 16, 2, 2048], P('grp', None, None, 'chan'), may hold values from -6 to 6
- flags: int32 [4, 128, 16, 2, 2048], P('grp', 'chan'), may hold values 0 or 1
- antennas: int32 [4, 2, 2048], P('grp'), may hold values from 0 to 63, as said below
- correlation: int32 [4, 4, 40], replicated, may hold values from -1 to 63, as said below
- gains_init: float32 [4, 2, 8, 128, 16, 64], P('grp', None, None, 'chan'), may hold values from -4 to 4
Outputs:
- final_jones_matrices: float32 [4, 2, 8, 128, 16, 64], P('grp', None, None, 'chan')
- consensus: float32 [4, 2, 8, 128, 16, 64], P('grp', None, None, 'chan')
- residual_vis: float32 [4, 2, 128, 16, 2, 2048], P('grp', None, 'chan')
Inputs may be any that keep to these rules, and one draw needn't show every extreme that they name: antennas[g, 0, b] and antennas[g, 1, b] are different slots. correlation[g, h, j] and correlation[h, g, j] are the slots in clusters g and h of one shared station, or both -1; the live entries of a list are a prefix of it and distinct; correlation[g, g] is all -1; each pair of clusters shares 40 // 2 to 40 stations, and some pair exactly 40.
All inputs are finite; a program needn't handle non-finite values. No bound on the sum of `flags` on one device may be relied on, other than what follows from the above.
Results may differ from a plain program's by a relative error of at most 0.0003.
Values sent between devices are 32-bit elements; how exact they have to be, the bound alone decides.
No kernel may reach another device: no remote copies, remote signals or barrier semaphores. Data moves between devices by JAX's collectives and lax.ppermute only.
A program may use at most 64 MiB of HBM per device.

v0:
```python
import functools

import jax
import jax.numpy as jnp
import numpy as np
from jax import lax
from jax.experimental import pallas as pl
from jax.experimental.pallas import tpu as pltpu
from jax.sharding import Mesh, PartitionSpec as P

K, SI, ST, BL, CL, CH = 8, 16, 64, 2048, 4, 128
RHO = 128.0
F32, BF16 = jnp.float32, jnp.bfloat16
NT = (((1,), (1,)), ((), ()))
BC = 512
VM = pl.BlockSpec(memory_space=pltpu.VMEM)
SD = jax.ShapeDtypeStruct
CUBE = ("y", "c", "zl")
PLANE = ("y", "c")
CHAN = ("y", "zh", "zl", "c")


def inverse_gram():
    f = np.arange(CH, dtype=np.float64)
    x = (2 * f + 1) / CH - 1
    basis = np.stack([np.ones_like(x), x, 1.5 * x * x - 0.5], axis=1)
    return np.linalg.inv(basis.T @ basis)


GINV = inverse_gram()


def iota(shape, dim):
    return lax.broadcasted_iota(jnp.int32, shape, dim)


def position(y, z, c):
    return (2 * (y * 32 + z * 2 + c) + 1).astype(F32) * (1.0 / CH) - 1.0


def basis_value(n, x):
    return jnp.where(n == 0, 1.0, jnp.where(n == 1, x, jnp.where(n == 2, 1.5 * x * x - 0.5, 0.0)))


def weight_value(n, x):
    second = 1.5 * x * x - 0.5
    rows = [float(g[0]) + float(g[1]) * x + float(g[2]) * second for g in GINV]
    return jnp.where(n == 0, rows[0], jnp.where(n == 1, rows[1], jnp.where(n == 2, rows[2], 0.0)))


def cube_entry(value, j, q):
    x = position(q >> 5, lax.axis_index("zh") * 4 + ((q >> 2) & 3), (q >> 4) & 1)
    return jnp.where((j & 3) == (q & 3), value(j >> 2, x), 0.0)


def cube_down():
    return cube_entry(weight_value, iota((16, 128), 0), iota((16, 128), 1))


def plane_down():
    j, q = iota((48, 128), 0), iota((48, 128), 1)
    zl = (j * 43) >> 9
    j = j - zl * 12
    z = lax.axis_index("zh") * 4 + lax.axis_index("zl")
    same = ((j & 3) == (q & 3)) & (zl == ((q >> 2) & 3))
    return jnp.where(same, weight_value(j >> 2, position(q >> 5, z, (q >> 4) & 1)), 0.0)


def split3(x):
    hi=x.astype(BF16); r=x-hi.astype(F32); mid=r.astype(BF16); lo=(r-mid.astype(F32)).astype(BF16)
    return hi,mid,lo


def split2(x):
    hi=x.astype(BF16)
    return hi,(x-hi.astype(F32)).astype(BF16)


def onehot(ants, side, off):
    ids=ants[side:side+1, pl.ds(off,BC)]
    io=lax.broadcasted_iota(jnp.int32,(ST,BC),0)
    return jnp.where(io==ids,1.0,0.0).astype(BF16)


def gather(g3, oh, out):
    out[...]=jnp.dot(g3, jnp.concatenate([oh,oh,oh],0), preferred_element_type=F32)


def totals_body(gains, ants, m_ref, v_ref, ga2, gc2, x2, acc):
    g3=jnp.concatenate(split3(gains),1)
    acc[...]=jnp.zeros_like(acc)
    def chunk(c):
        off=c*BC; ga=ga2.at[c%2]; gc=gc2.at[c%2]; x_ref=x2.at[c%2]
        oa=onehot(ants,0,off); oc=onehot(ants,1,off)
        if c==0:
            gather(g3,oa,ga); gather(g3,oc,gc)
        if c+1<BL//BC:
            gather(g3,onehot(ants,0,off+BC),ga2.at[(c+1)%2]); gather(g3,onehot(ants,1,off+BC),gc2.at[(c+1)%2])
        for lt in range(BC//128):
            L=slice(lt*128,lt*128+128)
            D=slice(off+lt*128,off+lt*128+128)
            res=[[v_ref[r,t,:,D] for r in range(2)] for t in range(2)]
            for k in range(K):
                ra=slice(k*16,k*16+16); ia=slice(128+k*16,128+k*16+16)
                ar,ai,cr,ci=ga[ra,L],ga[ia,L],gc[ra,L],gc[ia,L]
                pr=ar*cr+ai*ci; pi=ai*cr-ar*ci
                for t in range(2):
                    mr=m_ref[0,t,k,:,D].astype(F32); mi=m_ref[1,t,k,:,D].astype(F32)
                    res[t][0]=res[t][0]-(pr*mr-pi*mi)
                    res[t][1]=res[t][1]-(pr*mi+pi*mr)
            for k in range(K):
                ra=slice(k*16,k*16+16); ia=slice(128+k*16,128+k*16+16)
                ar,ai,cr,ci=ga[ra,L],ga[ia,L],gc[ra,L],gc[ia,L]
                dd=0.0; qr=0.0; qi=0.0
                for t in range(2):
                    mr=m_ref[0,t,k,:,D].astype(F32); mi=m_ref[1,t,k,:,D].astype(F32)
                    rr,ri=res[t]
                    qr=qr+(rr*mr+ri*mi); qi=qi+(ri*mr-rr*mi)
                    dd=dd+(mr*mr+mi*mi)
                vals=((qr*cr-qi*ci, qr*ci+qi*cr, (cr*cr+ci*ci)*dd),
                      (qr*ar+qi*ai, qr*ai-qi*ar, (ar*ar+ai*ai)*dd))
                for s in range(2):
                    LL=slice(s*BC+lt*128,s*BC+lt*128+128)
                    for q in range(3):
                        h,l=split2(vals[s][q])
                        x_ref[q*128+k*16:q*128+k*16+16,LL]=h
                        x_ref[384+q*128+k*16:384+q*128+k*16+16,LL]=l
        oh2=jnp.concatenate([oa,oc],1)
        t=lax.dot_general(x_ref[...],oh2,NT,preferred_element_type=F32)
        acc[...]+=t[:384]+t[384:]
        return 0
    for c in range(BL//BC): chunk(c)
    den=acc[256:384,:]
    acc[0:256,:]=acc[0:256,:]+gains*jnp.concatenate([den,den],0)


def unpack(jp):
    return jnp.concatenate([jp[:, :ST], jp[:, ST:]], 0)


def pack(top, bottom):
    return jnp.concatenate([top, bottom], 1)


def pack_kernel(g_ref, out):
    out[...] = pack(g_ref[0:128, :], g_ref[128:256, :])


def merge(out, fit, tmp, ab):
    tmp[...] = fit
    for r in range(4):
        at = pl.ds(r, 32, stride=4)
        out[pl.ds(r, 32, stride=10), :] = tmp[at, :]
        out[pl.ds(4 + r, 32, stride=10), :] = ab[at, :]
    left = iota((32, 128), 1) < ST
    for p in range(2):
        out[pl.ds(8 + p, 32, stride=10), :] = jnp.where(
            left, ab[pl.ds(128 + 2 * p, 32, stride=4), :], ab[pl.ds(129 + 2 * p, 32, stride=4), :])


def copies(out, value, times):
    rows = value.shape[0]
    for i in range(times):
        out[i * rows:i * rows + rows, :] = value


def first_kernel(g_ref, ants, m_ref, v_ref, ab, ga, gc, x_ref, acc):
    totals_body(g_ref[...], ants, m_ref, v_ref, ga, gc, x_ref, acc)
    inv = 1.0 / (acc[256:384, :] + RHO)
    inv = pack(inv, inv)
    ab[0:128, :] = pack(acc[0:128, :], acc[128:256, :]) * inv
    ab[128:256, :] = RHO * inv


def mm(a, b):
    a0, a1, a2 = split3(a)
    b0, b1, b2 = split3(b)
    return jnp.dot(jnp.concatenate([a0, a0, a0, a1, a1, a2], 1), jnp.concatenate([b0, b1, b2, b0, b1, b0], 0),
                   preferred_element_type=F32)


def expand(coef):
    j, q = iota((128, 96), 1), iota((128, 96), 0)
    piece = j >> 4
    whole = cube_entry(basis_value, j & 15, q)
    high = whole.astype(BF16).astype(F32)
    rest = whole - high
    middle = rest.astype(BF16).astype(F32)
    up = jnp.where(piece < 3, high, jnp.where(piece < 5, middle, rest - middle)).astype(BF16)
    c0, c1, c2 = split3(coef)
    return jnp.dot(up, jnp.concatenate([c0, c1, c2, c0, c1, c0], 0), preferred_element_type=F32)


def plane_kernel(recv, out):
    copies(out, mm(plane_down(), recv[...]), 4)


def summed(recv, first, count):
    total = recv[first * 12:first * 12 + 12, :]
    for i in range(1, count):
        s = (first + i) * 12
        total = total + recv[s:s + 12, :]
    return jnp.concatenate([total, jnp.zeros((4, 128), F32)], 0)


def fit_kernel(count, recv, ab, out, zh, tmp):
    z = expand(summed(recv, 0, count))
    zh[...] = z
    merge(out, z, tmp, ab)


def coefficients(recv, t_ref, cnt):
    return averaged([summed(recv, h * 4, 4) for h in range(CL)], range(CL), t_ref, cnt)


def last_fit_kernel(recv, t_ref, cnt, out):
    out[...] = expand(coefficients(recv, t_ref, cnt))


def stepped(got, zh, ab, tmp, j_out):
    left = iota((32, 128), 1) < ST
    for r in range(4):
        at = pl.ds(r, 32, stride=4)
        two = got[pl.ds(8 + r // 2, 32, stride=10), :]
        turned = jnp.concatenate([two[:, ST:], two[:, :ST]], 1)
        slope = jnp.where(left, two, turned) if r % 2 == 0 else jnp.where(left, turned, two)
        tmp[at, :] = got[pl.ds(4 + r, 32, stride=10), :] + slope * zh[at, :]
        j_out[at, :] = ab[at, :] + ab[pl.ds(128 + r, 32, stride=4), :] * got[pl.ds(r, 32, stride=10), :]
    return mm(cube_down(), tmp[...])


def update_kernel(got, zh, ab, out, tmp, own):
    part = stepped(got, zh, ab, tmp, own)
    for h in range(CL):
        out[h * 144:h * 144 + 128, :] = own[...]
        out[h * 144 + 128:h * 144 + 144, :] = part


def second_update_kernel(got, zh, ab, part, j_out, tmp):
    copies(part, stepped(got, zh, ab, tmp, j_out)[0:12], 16)


def meet_kernel(recv, t_ref, cnt, out):
    copies(out, averaged([recv[h * 144 + 128:h * 144 + 144, :] for h in range(CL)], range(CL), t_ref, cnt)[0:12], 4)


def map_kernel(mine, theirs, own, ants, t_ref, cnt, kept):
    kept[...] = ants[...]
    shared = mine.shape[1]
    io = lax.broadcasted_iota(jnp.int32, (ST, shared), 0)
    eye = jnp.where(lax.broadcasted_iota(jnp.int32, (ST, ST), 0) == lax.broadcasted_iota(jnp.int32, (ST, ST), 1), 1.0, 0.0)
    zero = jnp.zeros((ST, ST), F32)
    total = jnp.zeros((8, ST), F32)
    ones = jnp.ones((8, shared), BF16)
    for h in range(CL):
        om = jnp.where(io == mine[h:h + 1, :], 1.0, 0.0).astype(BF16)
        ot = jnp.where(io == theirs[h:h + 1, :], 1.0, 0.0).astype(BF16)
        t = lax.dot_general(ot, om, NT, preferred_element_type=F32) + eye * own[h:h + 1, :]
        t_ref[h * 128:h * 128 + 128, :] = pack(jnp.concatenate([t, zero], 0), jnp.concatenate([zero, t], 0)).astype(BF16)
        total = total + lax.dot_general(ones, om, NT, preferred_element_type=F32)
    cnt[...] = 1.0 / (1.0 + pack(total, total))


def averaged(parts, clusters, t_ref, cnt):
    total = 0.0
    for x, h in zip(parts, clusters):
        t = t_ref[pl.ds(pl.multiple_of(h * 128, 128), 128), :]
        total = total + jnp.dot(jnp.concatenate(split3(x), 1), jnp.concatenate([t, t, t], 0), preferred_element_type=F32)
    return total * cnt[0:1, :]


def average_of(own, r1, r2, r3, t_ref, cnt):
    g = lax.axis_index("x")
    return averaged([own[...], r1[...], r2[...], r3[...]], [lax.rem(g + CL - s, CL) for s in range(CL)], t_ref, cnt)


def second_kernel(recv, t_ref, cnt, ants, m_ref, v_ref, ab, ga, gc, x_ref, acc):
    j1 = averaged([recv[h * 144:h * 144 + 128, :] for h in range(CL)], range(CL), t_ref, cnt)
    totals_body(unpack(j1), ants, m_ref, v_ref, ga, gc, x_ref, acc)
    inv = 1.0 / (acc[256:384, :] + RHO)
    inv = pack(inv, inv)
    ab[0:128, :] = (pack(acc[0:128, :], acc[128:256, :]) - RHO * j1) * inv
    ab[128:256, :] = (2.0 * RHO) * inv


def gate_kernel(x_ref, out):
    out[...] = x_ref[...]


def unpack_kernel(z_ref, out):
    out[...] = unpack(z_ref[...])


def residual_kernel(own, r1, r2, r3, t_ref, cnt, ants, m_ref, v_ref, rows, out, ga, gc):
    gains = unpack(average_of(own, r1, r2, r3, t_ref, cnt))
    rows[...] = gains
    g3 = jnp.concatenate(split3(gains), 1)
    def chunk(c,_):
        off=pl.multiple_of(c*BC,BC)
        gather(g3,onehot(ants,0,off),ga); gather(g3,onehot(ants,1,off),gc)
        for lt in range(BC//128):
            L=slice(lt*128,lt*128+128)
            D=pl.ds(pl.multiple_of(off+lt*128,128),128)
            res=[[v_ref[r,t,:,D] for r in range(2)] for t in range(2)]
            for k in range(K):
                ra=slice(k*16,k*16+16); ia=slice(128+k*16,128+k*16+16)
                ar,ai,cr,ci=ga[ra,L],ga[ia,L],gc[ra,L],gc[ia,L]
                pr=ar*cr+ai*ci; pi=ai*cr-ar*ci
                for t in range(2):
                    mr=m_ref[0,t,k,:,D].astype(F32); mi=m_ref[1,t,k,:,D].astype(F32)
                    res[t][0]=res[t][0]-(pr*mr-pi*mi)
                    res[t][1]=res[t][1]-(pr*mi+pi*mr)
            for t in range(2):
                for r in range(2): out[r,t,:,D]=res[t][r]
        return 0
    lax.fori_loop(0,BL//BC,chunk,0,unroll=4)


def kernel(body, outs, ins, scratch=(), flops=100000000, vmem=8, moved=1000000):
    return pl.pallas_call(
        body, out_shape=outs, in_specs=[VM] * ins,
        out_specs=(VM,) * len(outs) if isinstance(outs, tuple) else VM,
        scratch_shapes=list(scratch),
        compiler_params=pltpu.CompilerParams(vmem_limit_bytes=vmem * 1048576),
        cost_estimate=pl.CostEstimate(flops=flops, bytes_accessed=moved, transcendentals=0))


def on_device(visibilities, model, flags, antennas, correlation, gains_init):
    ants = antennas[0]
    gains = gains_init.reshape(2 * K * SI, ST)
    group = lax.axis_index("x")
    mine = lax.dynamic_index_in_dim(correlation, group, 0, keepdims=False)
    theirs = lax.dynamic_index_in_dim(correlation, group, 1, keepdims=False)
    own = jnp.broadcast_to(jnp.where(jnp.arange(CL) == group, 1.0, 0.0)[:, None], (CL, ST))
    full = SD((128, 128), F32)
    tile = pltpu.VMEM((128, 128), F32)
    exchange = functools.partial(lax.all_to_all, split_axis=0, concat_axis=0, tiled=True)
    scratch = [pltpu.VMEM((2, 256, BC), F32), pltpu.VMEM((2, 256, BC), F32), pltpu.VMEM((2, 768, 2 * BC), BF16), pltpu.VMEM((384, ST), F32)]
    spread = [pltpu.VMEM((256, BC), F32), pltpu.VMEM((256, BC), F32)]
    big = 2000000000
    wide = SD((320, 128), F32)
    pairs = SD((256, 128), F32)
    moments = SD((192, 128), F32)

    def other(j, s):
        return lax.ppermute(j, "x", [(i, (i + s) % CL) for i in range(CL)])

    def swap(x, axes, *shape):
        return exchange(x.reshape(*shape, 128), axes).reshape(-1, 128)

    got = swap(kernel(pack_kernel, full, 1, flops=20000000000, moved=20000000)(gains), PLANE, 8, 16)
    keep = flags[0, 0] == 0
    m = jnp.where(keep[None, None], model[0][:, :, 0], jnp.zeros((), BF16)).transpose(0, 3, 1, 2, 4)
    v = jnp.where(keep[None], visibilities[0][:, 0], 0.0).transpose(0, 2, 1, 3)
    tmap, cnt, ants = kernel(map_kernel, (SD((CL * 128, 128), BF16), SD((8, 128), F32), SD((2, BL), jnp.int32)), 4)(
        mine, theirs, own, ants)
    got, m, v, tmap, cnt, ants = lax.optimization_barrier((got, m, v, tmap, cnt, ants))
    got = swap(kernel(plane_kernel, moments, 1)(got), ("zh", "zl"), 16, 3, 4)
    ab = kernel(first_kernel, pairs, 4, scratch, big, 24)(gains, ants, m, v)

    got, ab = lax.optimization_barrier((got, ab))
    send, zh = kernel(functools.partial(fit_kernel, 16), (wide, full), 2, [tile])(got, ab)
    got = swap(send, CUBE, 32, 5, 2)
    recv = exchange(kernel(update_kernel, SD((576, 128), F32), 3, [tile, tile])(got, zh, ab), "x")
    part = kernel(meet_kernel, SD((48, 128), F32), 3)(recv, tmap, cnt)
    got = swap(part, "zh", 4, 3, 4)
    ab = kernel(second_kernel, pairs, 6, scratch, big, 24)(recv, tmap, cnt, ants, m, v)
    send, zh = kernel(functools.partial(fit_kernel, 4), (wide, full), 2, [tile])(got, ab)
    got = swap(send, CUBE, 32, 5, 2)
    part, j2 = kernel(second_update_kernel, (moments, full), 3, [tile])(got, zh, ab)
    got = swap(part, ("x", "zh"), 16, 3, 4)
    r2, r3 = other(j2, 2), other(j2, 3)
    cnt2 = kernel(gate_kernel, SD((8, 128), F32), 1)(cnt)
    z = kernel(last_fit_kernel, full, 3)(got, tmap, cnt)
    z = swap(z, CUBE, 32, 4)
    r1 = other(j2, 1)
    rows, res = kernel(residual_kernel, (SD((256, ST), F32), SD((2, 2, SI, BL), F32)), 9, spread, big, 24)(
        j2, r1, r2, r3, tmap, cnt2, ants, m, v)
    zrows = kernel(unpack_kernel, SD((256, ST), F32), 1)(z)
    shape = gains_init.shape
    return rows.reshape(shape), zrows.reshape(shape), res.transpose(0, 2, 1, 3)[None, :, None]


def solution(mesh):
    split = Mesh(mesh.devices.reshape(4, 4, 4, 4, 2), ("x", "y", "zh", "zl", "c"))
    return jax.shard_map(
        on_device,
        mesh=split,
        in_specs=(
            P("x", None, CHAN, None, None, None),
            P("x", None, None, CHAN, None, None, None),
            P("x", CHAN, None, None, None),
            P("x", None, None),
            P(),
            P("x", None, None, CHAN, None, None),
        ),
        out_specs=(
            P("x", None, None, CHAN, None, None),
            P("x", None, None, CHAN, None, None),
            P("x", None, CHAN, None, None, None),
        ),
        check_vma=False,
    )
```

profile of v0, /device:TPU:1, one launch (start us, length us, event | category | flops | bytes accessed | tf_op | source)
XLA Modules:
  0.0 142.2 jit_solution(5011674898687981660)
XLA Ops:
  0.6 0.0 copy-start
  0.6 0.0 copy-start.1
  0.7 0.9 copy-done.1
  1.6 0.7 shard_map.85
  2.3 10.1 %all-to-all-start = ((f32[8,16,128]{2,1,0:T(8,128)}), f32[8,16,128]{2,1,0:T(8,128)S(1)}, u32[]{:S(2)}, u32[]{:S(2)}) async-start(f32[8,16,128]{2,1,0:T(8,128)} %bitcast.1), calls=%async_computation | async-start | bytes 131072 | tf_op jit(solution)/shard_map/all_to_all | solution.py:349
  12.4 0.0 copy-done
  12.4 0.0 copy-done.5
  12.4 0.2 compare_bitcast_fusion
  12.6 0.1 copy.9
  12.6 0.0 copy-start.4
  12.6 0.0 copy-start.3
  12.7 0.0 copy-start.2
  12.7 3.0 %fusion.m_ref = bf16[2,2,8,16,2048]{4,3,2,1,0:T(8,128)(2,1)S(1)} fusion(bf16[1,2,8,1,16,2,2048]{6,5,4,3,2,1,0:T(2,128)(2,1)} %param.7, pred[16,2,2048]{2,0,1:T(8,128)(4,1)S(1)} %copy.9), kind=kLoop, calls=%fused_computation.1 | loop fusion | flops 1048576 | bytes 4259840 | tf_op jit(solution)/shard_map/transpose | solution.py:353
  15.7 0.0 copy-done.4
  15.7 0.3 fusion.1.v_ref
  16.1 0.1 broadcast_in_dim.52.own
  16.1 0.0 copy-done.3
  16.1 0.3 shard_map.86
  16.4 0.8 all-to-all-done
  17.2 0.8 shard_map.87
  18.1 10.8 %all-to-all-start.1 = ((f32[16,3,4,128]{3,2,1,0:T(4,128)}), f32[16,3,4,128]{3,2,1,0:T(4,128)S(1)}, u32[]{:S(2)}, u32[]{:S(2)}) async-start(f32[16,3,4,128]{3,2,1,0:T(4,128)} %bitcast.11), calls=%async_computation.1 | async-start | bytes 196608 | tf_op jit(solution)/shard_map/all_to_all | solution.py:349
  28.8 0.0 copy-done.2
  28.8 5.4 %shard_map.88.ab = f32[256,128]{1,0:T(8,128)S(1)} custom-call(f32[256,64]{1,0:T(8,128)S(1)} %bitcast.60, s32[2,2048]{1,0:T(2,128)S(1)} %get-tuple-element.26.ants, bf16[2,2,8,16,2048]{4,3,2,1,0:T(8,128)(2,1)S(1)} %fusion.m_ref, f32[2,2,16,2048]{3,2,1,0:T(8,128)S(1)} %fusion.1.v_ref), custom_call_target="tpu_custom_call" | custom-call | flops 2000000000 | bytes 1000000 | tf_op jit(solution)/shard_map/pallas_call | solution.py:359
  34.3 6.4 %all-to-all-done.1 = f32[16,3,4,128]{3,2,1,0:T(4,128)S(1)} async-done(((f32[16,3,4,128]{3,2,1,0:T(4,128)}), f32[16,3,4,128]{3,2,1,0:T(4,128)S(1)}, u32[]{:S(2)}, u32[]{:S(2)}) %all-to-all-start.1) | async-done | bytes 98336 | tf_op jit(solution)/shard_map/all_to_all | solution.py:349
  40.7 0.2 shard_map.89
  40.9 16.4 %all_to_all.46 = f32[32,5,2,128]{3,2,1,0:T(2,128)S(1)} all-to-all(f32[32,5,2,128]{3,2,1,0:T(2,128)S(1)} %bitcast.50), channel_id=1, replica_groups=mesh['x'=4,'y'=4,'zh'=4,'zl'=4,'c'=2] {'y','c','zl'}, dimensions={0} | all-to-all | bytes 327680 | tf_op jit(solution)/shard_map/all_to_all | solution.py:349
  57.3 0.2 shard_map.90
  57.5 9.6 %all_to_all.47 = f32[4,144,128]{2,1,0:T(8,128)S(1)} all-to-all(f32[4,144,128]{2,1,0:T(8,128)S(1)} %bitcast.46), channel_id=1, replica_groups=mesh['x'=4,'y'=4,'zh'=4,'zl'=4,'c'=2] {'x'}, dimensions={0} | all-to-all | bytes 589824 | tf_op jit(solution)/shard_map/all_to_all | solution.py:364
  67.1 0.8 shard_map.91
  67.9 4.6 %all-to-all-start.4 = ((f32[4,3,4,128]{3,2,1,0:T(4,128)}), f32[4,3,4,128]{3,2,1,0:T(4,128)S(1)}, u32[]{:S(2)}, u32[]{:S(2)}) async-start(f32[4,3,4,128]{3,2,1,0:T(4,128)} %bitcast.17), calls=%async_computation.4 | async-start | bytes 49152 | tf_op jit(solution)/shard_map/all_to_all | solution.py:349
  72.6 5.8 %shard_map.92.ab = f32[256,128]{1,0:T(8,128)S(1)} custom-call(f32[576,128]{1,0:T(8,128)S(1)} %bitcast.45, bf16[512,128]{1,0:T(8,128)(2,1)S(1)} %get-tuple-element.33.t_ref, f32[8,128]{1,0:T(8,128)S(1)} %get-tuple-element.34.cnt.x_ref, s32[2,2048]{1,0:T(2,128)S(1)} %get-tuple-element.26.ants, bf16[2,2,8,16,2048]{4,3,2,1,0:T(8,128)(2,1)S(1)} %fusion.m_ref, ...), custom_call_target="tpu_custom_call" | custom-call | flops 2000000000 | bytes 1000000 | tf_op jit(solution)/shard_map/pallas_call | solution.py:367
  78.4 5.7 %all-to-all-done.4 = f32[4,3,4,128]{3,2,1,0:T(4,128)S(1)} async-done(((f32[4,3,4,128]{3,2,1,0:T(4,128)}), f32[4,3,4,128]{3,2,1,0:T(4,128)S(1)}, u32[]{:S(2)}, u32[]{:S(2)}) %all-to-all-start.4) | async-done | bytes 24608 | tf_op jit(solution)/shard_map/all_to_all | solution.py:349
  84.1 0.2 shard_map.93
  84.3 16.0 %all_to_all.48 = f32[32,5,2,128]{3,2,1,0:T(2,128)S(1)} all-to-all(f32[32,5,2,128]{3,2,1,0:T(2,128)S(1)} %bitcast.51), channel_id=1, replica_groups=mesh['x'=4,'y'=4,'zh'=4,'zl'=4,'c'=2] {'y','c','zl'}, dimensions={0} | all-to-all | bytes 327680 | tf_op jit(solution)/shard_map/all_to_all | solution.py:349
  100.3 0.2 shard_map.94
  100.5 19.9 %all_to_all.49 = f32[16,3,4,128]{3,2,1,0:T(4,128)S(1)} all-to-all(f32[16,3,4,128]{3,2,1,0:T(4,128)S(1)} %bitcast.53), channel_id=1, replica_groups=mesh['x'=4,'y'=4,'zh'=4,'zl'=4,'c'=2] {'x','zh'}, dimensions={0} | all-to-all | bytes 196608 | tf_op jit(solution)/shard_map/all_to_all | solution.py:349
  120.5 1.0 shard_map.97
  121.4 6.4 %all-to-all-start.7 = ((f32[32,4,128]{2,1,0:T(4,128)}), f32[32,4,128]{2,1,0:T(4,128)S(1)}, u32[]{:S(2)}, u32[]{:S(2)}) async-start(f32[32,4,128]{2,1,0:T(4,128)} %bitcast.25), calls=%async_computation.7 | async-start | bytes 131072 | tf_op jit(solution)/shard_map/all_to_all | solution.py:349
  127.8 1.9 %collective-permute-start = (f32[128,128]{1,0:T(8,128)S(1)}, f32[128,128]{1,0:T(8,128)S(1)}, u32[]{:S(2)}, u32[]{:S(2)}) collective-permute-start(f32[128,128]{1,0:T(8,128)S(1)} %get-tuple-element.37.own), channel_id=1, source_target_pairs={{0,128},{128,256},{256,384},{384,0},{1,129},{129,257},{257,385},{3... | collective-permute-start | bytes 196616 | tf_op jit(solution)/shard_map/ppermute | solution.py:346
  129.8 3.7 %collective-permute-start.1 = (f32[128,128]{1,0:T(8,128)S(1)}, f32[128,128]{1,0:T(8,128)S(1)}, u32[]{:S(2)}, u32[]{:S(2)}) collective-permute-start(f32[128,128]{1,0:T(8,128)S(1)} %get-tuple-element.37.own), channel_id=1, source_target_pairs={{0,256},{128,384},{256,0},{384,128},{1,257},{129,385},{257,1},{385... | collective-permute-start | bytes 196616 | tf_op jit(solution)/shard_map/ppermute | solution.py:346
  133.4 2.8 %collective-permute-start.2 = (f32[128,128]{1,0:T(8,128)S(1)}, f32[128,128]{1,0:T(8,128)S(1)}, u32[]{:S(2)}, u32[]{:S(2)}) collective-permute-start(f32[128,128]{1,0:T(8,128)S(1)} %get-tuple-element.37.own), channel_id=1, source_target_pairs={{0,384},{128,0},{256,128},{384,256},{1,385},{129,1},{257,129},{385... | collective-permute-start | bytes 196616 | tf_op jit(solution)/shard_map/ppermute | solution.py:346
  136.3 0.0 collective-permute-done.r1
  136.3 0.3 collective-permute-done.1.r2
  136.6 1.9 %collective-permute-done.2.r3 = f32[128,128]{1,0:T(8,128)S(1)} collective-permute-done((f32[128,128]{1,0:T(8,128)S(1)}, f32[128,128]{1,0:T(8,128)S(1)}, u32[]{:S(2)}, u32[]{:S(2)}) %collective-permute-start.2) | collective-permute-done | bytes 65568 | tf_op jit(solution)/shard_map/ppermute | solution.py:346
  138.5 1.8 %shard_map.96 = (f32[256,64]{1,0:T(8,128)}, f32[2,2,16,2048]{3,2,1,0:T(8,128)S(1)}) custom-call(f32[128,128]{1,0:T(8,128)S(1)} %get-tuple-element.37.own, f32[128,128]{1,0:T(8,128)S(1)} %collective-permute-done.r1, f32[128,128]{1,0:T(8,128)S(1)} %collective-permute-done.1.r2, f32[128,128]{1,0:T(8,128)S(1)} %collective-permute-done.2.r3, ...), custom_call_target="tpu_custom_call" | custom-call | flops 2000000000 | bytes 1000000 | tf_op jit(solution)/shard_map/pallas_call | solution.py:377
  140.3 1.2 copy.15
  141.5 0.0 all-to-all-done.7
  141.5 0.7 shard_map.98
  (5 shorter events, 0.0 us)
Async XLA Ops:
  0.6 11.7 %copy-start = (s32[4,4,40]{2,1,0:T(4,128)S(1)}, s32[4,4,40]{2,1,0:T(4,128)}, u32[]{:S(2)}) copy-start(s32[4,4,40]{2,1,0:T(4,128)} %param.10) | copy-start | bytes 7684
  0.6 0.9 copy-start.1
  1.6 10.8 %copy-start.5 = (s32[1,1,16,2,2048]{4,3,2,1,0:T(2,128)S(1)}, s32[1,1,16,2,2048]{4,3,2,1,0:T(2,128)}, u32[]{:S(2)}) copy-start(s32[1,1,16,2,2048]{4,3,2,1,0:T(2,128)} %param.8) | copy-start | bytes 786436
  2.3 15.0 %all-to-all-start = ((f32[8,16,128]{2,1,0:T(8,128)}), f32[8,16,128]{2,1,0:T(8,128)S(1)}, u32[]{:S(2)}, u32[]{:S(2)}) async-start(f32[8,16,128]{2,1,0:T(8,128)} %bitcast.1), calls=%async_computation | async-start | bytes 131072 | tf_op jit(solution)/shard_map/all_to_all | solution.py:349
  12.6 3.0 %copy-start.4 = (f32[1,2,1,16,2,2048]{5,4,3,2,1,0:T(2,128)S(1)}, f32[1,2,1,16,2,2048]{5,4,3,2,1,0:T(2,128)}, u32[]{:S(2)}) copy-start(f32[1,2,1,16,2,2048]{5,4,3,2,1,0:T(2,128)} %param.6) | copy-start | bytes 1572868
  12.6 3.5 %copy-start.3 = (s32[1,2,2048]{2,1,0:T(2,128)S(1)}, s32[1,2,2048]{2,1,0:T(2,128)}, u32[]{:S(2)}) copy-start(s32[1,2,2048]{2,1,0:T(2,128)} %param.9) | copy-start | bytes 49156
  12.7 16.2 %copy-start.2 = (f32[1,2,8,1,16,64]{5,4,3,2,1,0:T(8,128)S(1)}, f32[1,2,8,1,16,64]{5,4,3,2,1,0:T(8,128)}, u32[]{:S(2)}) copy-start(f32[1,2,8,1,16,64]{5,4,3,2,1,0:T(8,128)} %param.11) | copy-start | bytes 196612
  18.1 22.6 %all-to-all-start.1 = ((f32[16,3,4,128]{3,2,1,0:T(4,128)}), f32[16,3,4,128]{3,2,1,0:T(4,128)S(1)}, u32[]{:S(2)}, u32[]{:S(2)}) async-start(f32[16,3,4,128]{3,2,1,0:T(4,128)} %bitcast.11), calls=%async_computation.1 | async-start | bytes 196608 | tf_op jit(solution)/shard_map/all_to_all | solution.py:349
  67.9 16.1 %all-to-all-start.4 = ((f32[4,3,4,128]{3,2,1,0:T(4,128)}), f32[4,3,4,128]{3,2,1,0:T(4,128)S(1)}, u32[]{:S(2)}, u32[]{:S(2)}) async-start(f32[4,3,4,128]{3,2,1,0:T(4,128)} %bitcast.17), calls=%async_computation.4 | async-start | bytes 49152 | tf_op jit(solution)/shard_map/all_to_all | solution.py:349
  121.4 20.0 %all-to-all-start.7 = ((f32[32,4,128]{2,1,0:T(4,128)}), f32[32,4,128]{2,1,0:T(4,128)S(1)}, u32[]{:S(2)}, u32[]{:S(2)}) async-start(f32[32,4,128]{2,1,0:T(4,128)} %bitcast.25), calls=%async_computation.7 | async-start | bytes 131072 | tf_op jit(solution)/shard_map/all_to_all | solution.py:349
  127.8 8.5 %collective-permute-start = (f32[128,128]{1,0:T(8,128)S(1)}, f32[128,128]{1,0:T(8,128)S(1)}, u32[]{:S(2)}, u32[]{:S(2)}) collective-permute-start(f32[128,128]{1,0:T(8,128)S(1)} %get-tuple-element.37.own), channel_id=1, source_target_pairs={{0,128},{128,256},{256,384},{384,0},{1,129},{129,257},{257,385},{3... | collective-permute-start | bytes 196616 | tf_op jit(solution)/shard_map/ppermute | solution.py:346
  129.8 6.8 %collective-permute-start.1 = (f32[128,128]{1,0:T(8,128)S(1)}, f32[128,128]{1,0:T(8,128)S(1)}, u32[]{:S(2)}, u32[]{:S(2)}) collective-permute-start(f32[128,128]{1,0:T(8,128)S(1)} %get-tuple-element.37.own), channel_id=1, source_target_pairs={{0,256},{128,384},{256,0},{384,128},{1,257},{129,385},{257,1},{385... | collective-permute-start | bytes 196616 | tf_op jit(solution)/shard_map/ppermute | solution.py:346
  133.4 5.1 %collective-permute-start.2 = (f32[128,128]{1,0:T(8,128)S(1)}, f32[128,128]{1,0:T(8,128)S(1)}, u32[]{:S(2)}, u32[]{:S(2)}) collective-permute-start(f32[128,128]{1,0:T(8,128)S(1)} %get-tuple-element.37.own), channel_id=1, source_target_pairs={{0,384},{128,0},{256,128},{384,256},{1,385},{129,1},{257,129},{385... | collective-permute-start | bytes 196616 | tf_op jit(solution)/shard_map/ppermute | solution.py:346
where the time goes:
time: 144 us; the launch traced here: 142 us
  blocking collectives  61.9 us (43%)
  starting transfers between devices  40.3 us (28%)
  Pallas kernels  18.2 us (13%)
  waiting for transfers between devices  15.1 us (10%)
  other arithmetic  3.51 us (2%)
  local copies, waits for them, and re-layouts  2.28 us (2%)
    all_to_all x3, blocking collectives, swap(): return exchange(x.reshape(*shape, 128), axes).reshape(-1, 128)  52.3 us
    all_to_all x4, starting transfers between devices, swap(): return exchange(x.reshape(*shape, 128), axes).reshape(-1, 128)  31.9 us
    all_to_all x4, waiting for transfers between devices, swap(): return exchange(x.reshape(*shape, 128), axes).reshape(-1, 128)  12.9 us
    all_to_all x1, blocking collectives, on_device(): exchange(kernel(update_kernel, SD((576, 128), F32), 3, [tile, tile])(got,...  9.6 us
    ppermute x3, starting transfers between devices, other(): return lax.ppermute(j, 'x', [(i, (i + s) % CL) for i in range(CL)])  8.41 us
    pallas_call x1, Pallas kernels, on_device(): kernel(second_kernel, pairs, 6, scratch, big, 24)  5.77 us
    pallas_call x1, Pallas kernels, on_device(): ab = kernel(first_kernel, pairs, 4, scratch, big, 24)(gains, ants, m, v)  5.44 us
    transpose x1, other arithmetic, on_device(): jnp.where(keep[None, None], model[0][:, :, 0], jnp.zeros((), BF16))  3.01 us
  transfers between devices with their start and end apart: 7, of which 5 were waited for; matrix products, arithmetic and copies ran while one was open for 3% of the time, Pallas kernels for 9%

commit v1 on v0

--- a/solution.py
+++ b/solution.py
@@ -86,15 +86,16 @@
     out[...]=jnp.dot(g3, jnp.concatenate([oh,oh,oh],0), preferred_element_type=F32)
 
 
-def totals_body(gains, ants, m_ref, v_ref, ga2, gc2, x2, acc):
+def totals_body(gains, ants, m_ref, v_ref, ga2, gc2, x2, acc, low=0, high=BL//BC):
     g3=jnp.concatenate(split3(gains),1)
-    acc[...]=jnp.zeros_like(acc)
+    if low==0:
+        acc[...]=jnp.zeros_like(acc)
     def chunk(c):
         off=c*BC; ga=ga2.at[c%2]; gc=gc2.at[c%2]; x_ref=x2.at[c%2]
         oa=onehot(ants,0,off); oc=onehot(ants,1,off)
-        if c==0:
+        if c==low:
             gather(g3,oa,ga); gather(g3,oc,gc)
-        if c+1<BL//BC:
+        if c+1<high:
             gather(g3,onehot(ants,0,off+BC),ga2.at[(c+1)%2]); gather(g3,onehot(ants,1,off+BC),gc2.at[(c+1)%2])
         for lt in range(BC//128):
             L=slice(lt*128,lt*128+128)
@@ -129,7 +130,9 @@
         t=lax.dot_general(x_ref[...],oh2,NT,preferred_element_type=F32)
         acc[...]+=t[:384]+t[384:]
         return 0
-    for c in range(BL//BC): chunk(c)
+    for c in range(low,high): chunk(c)
+    if high<BL//BC:
+        return
     den=acc[256:384,:]
     acc[0:256,:]=acc[0:256,:]+gains*jnp.concatenate([den,den],0)
 
@@ -164,8 +167,13 @@
         out[i * rows:i * rows + rows, :] = value
 
 
-def first_kernel(g_ref, ants, m_ref, v_ref, ab, ga, gc, x_ref, acc):
-    totals_body(g_ref[...], ants, m_ref, v_ref, ga, gc, x_ref, acc)
+def early_kernel(g_ref, ants, m_ref, v_ref, sums, ga, gc, x_ref):
+    totals_body(g_ref[...], ants, m_ref, v_ref, ga, gc, x_ref, sums, 0, 1)
+
+
+def first_kernel(g_ref, ants, m_ref, v_ref, sums, ab, ga, gc, x_ref, acc):
+    acc[...] = sums[...]
+    totals_body(g_ref[...], ants, m_ref, v_ref, ga, gc, x_ref, acc, 1)
     inv = 1.0 / (acc[256:384, :] + RHO)
     inv = pack(inv, inv)
     ab[0:128, :] = pack(acc[0:128, :], acc[128:256, :]) * inv
@@ -342,8 +350,8 @@
     pairs = SD((256, 128), F32)
     moments = SD((192, 128), F32)
 
-    def other(j, s):
-        return lax.ppermute(j, "x", [(i, (i + s) % CL) for i in range(CL)])
+    def others(j):
+        return [lax.ppermute(j, "x", [(i, (i + s) % CL) for i in range(CL)]) for s in range(1, CL)]
 
     def swap(x, axes, *shape):
         return exchange(x.reshape(*shape, 128), axes).reshape(-1, 128)
@@ -354,9 +362,10 @@
     v = jnp.where(keep[None], visibilities[0][:, 0], 0.0).transpose(0, 2, 1, 3)
     tmap, cnt, ants = kernel(map_kernel, (SD((CL * 128, 128), BF16), SD((8, 128), F32), SD((2, BL), jnp.int32)), 4)(
         mine, theirs, own, ants)
-    got, m, v, tmap, cnt, ants = lax.optimization_barrier((got, m, v, tmap, cnt, ants))
+    sums = kernel(early_kernel, SD((384, ST), F32), 4, scratch[:3], big // 4, 24)(gains, ants, m, v)
+    got, m, v, tmap, cnt, ants, sums = lax.optimization_barrier((got, m, v, tmap, cnt, ants, sums))
     got = swap(kernel(plane_kernel, moments, 1)(got), ("zh", "zl"), 16, 3, 4)
-    ab = kernel(first_kernel, pairs, 4, scratch, big, 24)(gains, ants, m, v)
+    ab = kernel(first_kernel, pairs, 5, scratch, big, 24)(gains, ants, m, v, sums)
 
     got, ab = lax.optimization_barrier((got, ab))
     send, zh = kernel(functools.partial(fit_kernel, 16), (wide, full), 2, [tile])(got, ab)
@@ -369,14 +378,12 @@
     got = swap(send, CUBE, 32, 5, 2)
     part, j2 = kernel(second_update_kernel, (moments, full), 3, [tile])(got, zh, ab)
     got = swap(part, ("x", "zh"), 16, 3, 4)
-    r2, r3 = other(j2, 2), other(j2, 3)
+    d2 = others(j2)
     cnt2 = kernel(gate_kernel, SD((8, 128), F32), 1)(cnt)
+    rows, res = kernel(residual_kernel, (SD((256, ST), F32), SD((2, 2, SI, BL), F32)), 9, spread, big, 24)(
+        j2, *d2, tmap, cnt2, ants, m, v)
     z = kernel(last_fit_kernel, full, 3)(got, tmap, cnt)
-    z = swap(z, CUBE, 32, 4)
-    r1 = other(j2, 1)
-    rows, res = kernel(residual_kernel, (SD((256, ST), F32), SD((2, 2, SI, BL), F32)), 9, spread, big, 24)(
-        j2, r1, r2, r3, tmap, cnt2, ants, m, v)
-    zrows = kernel(unpack_kernel, SD((256, ST), F32), 1)(z)
+    zrows = kernel(unpack_kernel, SD((256, ST), F32), 1)(swap(z, CUBE, 32, 4))
     shape = gains_init.shape
     return rows.reshape(shape), zrows.reshape(shape), res.transpose(0, 2, 1, 3)[None, :, None]
 

time: 144 us -> 145 us (level)
    pallas_call x2 -> x3, Pallas kernels: 6.17 us -> 6.34 us  [the longest x1 4.13 us: on_device(): kernel(first_kernel, pairs, 5, scratch, big, 24)(gains, ants, m, v, sums)]
  transfers between devices with their start and end apart: 7 -> 7, of which waited for: 5 -> 4; matrix products, arithmetic and copies ran while one was open for 3% -> 3% of each run, Pallas kernels for 9% -> 9%
where the time goes in v1:
time: 145 us; the launch traced here: 144 us
  blocking collectives  62.7 us (43%)
  starting transfers between devices  40.3 us (28%)
  Pallas kernels  18.4 us (13%)
  waiting for transfers between devices  15.7 us (11%)
  other arithmetic  3.51 us (2%)
  local copies, waits for them, and re-layouts  2.28 us (2%)
    all_to_all x3, blocking collectives, swap(): return exchange(x.reshape(*shape, 128), axes).reshape(-1, 128)  53.1 us
    all_to_all x4, starting transfers between devices, swap(): return exchange(x.reshape(*shape, 128), axes).reshape(-1, 128)  31.9 us
    all_to_all x4, waiting for transfers between devices, swap(): return exchange(x.reshape(*shape, 128), axes).reshape(-1, 128)  13.5 us
    all_to_all x1, blocking collectives, on_device(): exchange(kernel(update_kernel, SD((576, 128), F32), 3, [tile, tile])(got,...  9.63 us
    ppermute x3, starting transfers between devices, others(): lax.ppermute(j, 'x', [(i, (i + s) % CL) for i in range(CL)])  8.41 us
    pallas_call x1, Pallas kernels, on_device(): kernel(second_kernel, pairs, 6, scratch, big, 24)  5.76 us
    pallas_call x1, Pallas kernels, on_device(): kernel(first_kernel, pairs, 5, scratch, big, 24)(gains, ants, m, v, sums)  4.13 us
    transpose x1, other arithmetic, on_device(): jnp.where(keep[None, None], model[0][:, :, 0], jnp.zeros((), BF16))  3.01 us
  transfers between devices with their start and end apart: 7, of which 4 were waited for; matrix products, arithmetic and copies ran while one was open for 3% of the time, Pallas kernels for 9%

profile of v1, /device:TPU:1, one launch (start us, length us, event | category | flops | bytes accessed | tf_op | source)
XLA Modules:
  0.0 143.7 jit_solution(107754008696141486)
XLA Ops:
  0.6 0.0 copy-start
  0.6 0.0 copy-start.1
  0.7 0.9 copy-done.1
  1.6 0.7 shard_map.85
  2.3 10.1 %all-to-all-start = ((f32[8,16,128]{2,1,0:T(8,128)}), f32[8,16,128]{2,1,0:T(8,128)S(1)}, u32[]{:S(2)}, u32[]{:S(2)}) async-start(f32[8,16,128]{2,1,0:T(8,128)} %bitcast.1), calls=%async_computation | async-start | bytes 131072 | tf_op jit(solution)/shard_map/all_to_all | solution.py:357
  12.4 0.0 copy-done
  12.4 0.0 copy-done.5
  12.4 0.2 compare_bitcast_fusion
  12.6 0.1 copy.9
  12.6 0.0 copy-start.4
  12.6 0.0 copy-start.3
  12.7 0.0 copy-start.2
  12.7 3.0 %fusion.m_ref = bf16[2,2,8,16,2048]{4,3,2,1,0:T(8,128)(2,1)S(1)} fusion(bf16[1,2,8,1,16,2,2048]{6,5,4,3,2,1,0:T(2,128)(2,1)} %param.7, pred[16,2,2048]{2,0,1:T(8,128)(4,1)S(1)} %copy.9), kind=kLoop, calls=%fused_computation.1 | loop fusion | flops 1048576 | bytes 4259840 | tf_op jit(solution)/shard_map/transpose | solution.py:361
  15.7 0.0 copy-done.4
  15.7 0.3 fusion.1.v_ref
  16.1 0.1 broadcast_in_dim.52.own
  16.1 0.3 shard_map.86
  16.4 0.0 copy-done.2
  16.4 1.5 %shard_map.87.sums = f32[384,64]{1,0:T(8,128)S(1)} custom-call(f32[256,64]{1,0:T(8,128)S(1)} %bitcast.53, s32[2,2048]{1,0:T(2,128)S(1)} %get-tuple-element.27.ants, bf16[2,2,8,16,2048]{4,3,2,1,0:T(8,128)(2,1)S(1)} %fusion.m_ref, f32[2,2,16,2048]{3,2,1,0:T(8,128)S(1)} %fusion.1.v_ref), custom_call_target="tpu_custom_call" | custom-call | flops 500000000 | bytes 1000000 | tf_op jit(solution)/shard_map/pallas_call | solution.py:365
  17.9 0.0 all-to-all-done
  17.9 0.8 shard_map.88
  18.7 10.8 %all-to-all-start.1 = ((f32[16,3,4,128]{3,2,1,0:T(4,128)}), f32[16,3,4,128]{3,2,1,0:T(4,128)S(1)}, u32[]{:S(2)}, u32[]{:S(2)}) async-start(f32[16,3,4,128]{3,2,1,0:T(4,128)} %bitcast.11), calls=%async_computation.1 | async-start | bytes 196608 | tf_op jit(solution)/shard_map/all_to_all | solution.py:357
  29.5 4.1 %shard_map.89.ab = f32[256,128]{1,0:T(8,128)S(1)} custom-call(f32[256,64]{1,0:T(8,128)S(1)} %bitcast.54, s32[2,2048]{1,0:T(2,128)S(1)} %get-tuple-element.27.ants, bf16[2,2,8,16,2048]{4,3,2,1,0:T(8,128)(2,1)S(1)} %fusion.m_ref, f32[2,2,16,2048]{3,2,1,0:T(8,128)S(1)} %fusion.1.v_ref, f32[384,64]{1,0:T(8,128)S(1)} %shard_map.87.sums), custom_call_target="tpu_custom_call" | custom-call | flops 2000000000 | bytes 1000000 | tf_op jit(solution)/shard_map/pallas_call | solution.py:368
  33.6 7.8 %all-to-all-done.1 = f32[16,3,4,128]{3,2,1,0:T(4,128)S(1)} async-done(((f32[16,3,4,128]{3,2,1,0:T(4,128)}), f32[16,3,4,128]{3,2,1,0:T(4,128)S(1)}, u32[]{:S(2)}, u32[]{:S(2)}) %all-to-all-start.1) | async-done | bytes 98336 | tf_op jit(solution)/shard_map/all_to_all | solution.py:357
  41.4 0.2 shard_map.90
  41.7 17.1 %all_to_all.46 = f32[32,5,2,128]{3,2,1,0:T(2,128)S(1)} all-to-all(f32[32,5,2,128]{3,2,1,0:T(2,128)S(1)} %bitcast.50), channel_id=1, replica_groups=mesh['x'=4,'y'=4,'zh'=4,'zl'=4,'c'=2] {'y','c','zl'}, dimensions={0} | all-to-all | bytes 327680 | tf_op jit(solution)/shard_map/all_to_all | solution.py:357
  58.8 0.2 shard_map.91
  59.0 9.6 %all_to_all.47 = f32[4,144,128]{2,1,0:T(8,128)S(1)} all-to-all(f32[4,144,128]{2,1,0:T(8,128)S(1)} %bitcast.46), channel_id=1, replica_groups=mesh['x'=4,'y'=4,'zh'=4,'zl'=4,'c'=2] {'x'}, dimensions={0} | all-to-all | bytes 589824 | tf_op jit(solution)/shard_map/all_to_all | solution.py:373
  68.7 0.8 shard_map.92
  69.5 4.6 %all-to-all-start.4 = ((f32[4,3,4,128]{3,2,1,0:T(4,128)}), f32[4,3,4,128]{3,2,1,0:T(4,128)S(1)}, u32[]{:S(2)}, u32[]{:S(2)}) async-start(f32[4,3,4,128]{3,2,1,0:T(4,128)} %bitcast.17), calls=%async_computation.4 | async-start | bytes 49152 | tf_op jit(solution)/shard_map/all_to_all | solution.py:357
  74.1 5.8 %shard_map.93.ab = f32[256,128]{1,0:T(8,128)S(1)} custom-call(f32[576,128]{1,0:T(8,128)S(1)} %bitcast.45, bf16[512,128]{1,0:T(8,128)(2,1)S(1)} %get-tuple-element.35.t_ref, f32[8,128]{1,0:T(8,128)S(1)} %get-tuple-element.36.cnt.x_ref, s32[2,2048]{1,0:T(2,128)S(1)} %get-tuple-element.27.ants, bf16[2,2,8,16,2048]{4,3,2,1,0:T(8,128)(2,1)S(1)} %fusion.m_ref, ...), custom_call_target="tpu_custom_call" | custom-call | flops 2000000000 | bytes 1000000 | tf_op jit(solution)/shard_map/pallas_call | solution.py:376
  79.9 5.7 %all-to-all-done.4 = f32[4,3,4,128]{3,2,1,0:T(4,128)S(1)} async-done(((f32[4,3,4,128]{3,2,1,0:T(4,128)}), f32[4,3,4,128]{3,2,1,0:T(4,128)S(1)}, u32[]{:S(2)}, u32[]{:S(2)}) %all-to-all-start.4) | async-done | bytes 24608 | tf_op jit(solution)/shard_map/all_to_all | solution.py:357
  85.6 0.2 shard_map.94
  85.8 16.0 %all_to_all.48 = f32[32,5,2,128]{3,2,1,0:T(2,128)S(1)} all-to-all(f32[32,5,2,128]{3,2,1,0:T(2,128)S(1)} %bitcast.51), channel_id=1, replica_groups=mesh['x'=4,'y'=4,'zh'=4,'zl'=4,'c'=2] {'y','c','zl'}, dimensions={0} | all-to-all | bytes 327680 | tf_op jit(solution)/shard_map/all_to_all | solution.py:357
  101.8 0.2 shard_map.95
  102.0 19.9 %all_to_all.49 = f32[16,3,4,128]{3,2,1,0:T(4,128)S(1)} all-to-all(f32[16,3,4,128]{3,2,1,0:T(4,128)S(1)} %bitcast.56), channel_id=1, replica_groups=mesh['x'=4,'y'=4,'zh'=4,'zl'=4,'c'=2] {'x','zh'}, dimensions={0} | all-to-all | bytes 196608 | tf_op jit(solution)/shard_map/all_to_all | solution.py:357
  122.0 1.0 shard_map.98
  122.9 6.4 %all-to-all-start.7 = ((f32[32,4,128]{2,1,0:T(4,128)}), f32[32,4,128]{2,1,0:T(4,128)S(1)}, u32[]{:S(2)}, u32[]{:S(2)}) async-start(f32[32,4,128]{2,1,0:T(4,128)} %bitcast.25), calls=%async_computation.7 | async-start | bytes 131072 | tf_op jit(solution)/shard_map/all_to_all | solution.py:357
  129.3 1.9 %collective-permute-start = (f32[128,128]{1,0:T(8,128)S(1)}, f32[128,128]{1,0:T(8,128)S(1)}, u32[]{:S(2)}, u32[]{:S(2)}) collective-permute-start(f32[128,128]{1,0:T(8,128)S(1)} %get-tuple-element.39.own), channel_id=1, source_target_pairs={{0,128},{128,256},{256,384},{384,0},{1,129},{129,257},{257,385},{3... | collective-permute-start | bytes 196616 | tf_op jit(solution)/shard_map/ppermute | solution.py:354
  131.3 3.7 %collective-permute-start.1 = (f32[128,128]{1,0:T(8,128)S(1)}, f32[128,128]{1,0:T(8,128)S(1)}, u32[]{:S(2)}, u32[]{:S(2)}) collective-permute-start(f32[128,128]{1,0:T(8,128)S(1)} %get-tuple-element.39.own), channel_id=1, source_target_pairs={{0,256},{128,384},{256,0},{384,128},{1,257},{129,385},{257,1},{385... | collective-permute-start | bytes 196616 | tf_op jit(solution)/shard_map/ppermute | solution.py:354
  134.9 2.8 %collective-permute-start.2 = (f32[128,128]{1,0:T(8,128)S(1)}, f32[128,128]{1,0:T(8,128)S(1)}, u32[]{:S(2)}, u32[]{:S(2)}) collective-permute-start(f32[128,128]{1,0:T(8,128)S(1)} %get-tuple-element.39.own), channel_id=1, source_target_pairs={{0,384},{128,0},{256,128},{384,256},{1,385},{129,1},{257,129},{385... | collective-permute-start | bytes 196616 | tf_op jit(solution)/shard_map/ppermute | solution.py:354
  137.8 0.0 collective-permute-done.r1
  137.8 0.3 collective-permute-done.1.r2
  138.1 1.9 %collective-permute-done.2.r3 = f32[128,128]{1,0:T(8,128)S(1)} collective-permute-done((f32[128,128]{1,0:T(8,128)S(1)}, f32[128,128]{1,0:T(8,128)S(1)}, u32[]{:S(2)}, u32[]{:S(2)}) %collective-permute-start.2) | collective-permute-done | bytes 65568 | tf_op jit(solution)/shard_map/ppermute | solution.py:354
  140.0 1.8 %shard_map.97 = (f32[256,64]{1,0:T(8,128)}, f32[2,2,16,2048]{3,2,1,0:T(8,128)S(1)}) custom-call(f32[128,128]{1,0:T(8,128)S(1)} %get-tuple-element.39.own, f32[128,128]{1,0:T(8,128)S(1)} %collective-permute-done.r1, f32[128,128]{1,0:T(8,128)S(1)} %collective-permute-done.1.r2, f32[128,128]{1,0:T(8,128)S(1)} %collective-permute-done.2.r3, ...), custom_call_target="tpu_custom_call" | custom-call | flops 2000000000 | bytes 1000000 | tf_op jit(solution)/shard_map/pallas_call | solution.py:383
  141.7 1.2 copy.15
  142.9 0.0 all-to-all-done.7
  142.9 0.7 shard_map.99
  (6 shorter events, 0.0 us)
Async XLA Ops:
  0.6 11.7 %copy-start = (s32[4,4,40]{2,1,0:T(4,128)S(1)}, s32[4,4,40]{2,1,0:T(4,128)}, u32[]{:S(2)}) copy-start(s32[4,4,40]{2,1,0:T(4,128)} %param.10) | copy-start | bytes 7684
  0.6 0.9 copy-start.1
  1.6 10.8 %copy-start.5 = (s32[1,1,16,2,2048]{4,3,2,1,0:T(2,128)S(1)}, s32[1,1,16,2,2048]{4,3,2,1,0:T(2,128)}, u32[]{:S(2)}) copy-start(s32[1,1,16,2,2048]{4,3,2,1,0:T(2,128)} %param.8) | copy-start | bytes 786436
  2.3 15.6 %all-to-all-start = ((f32[8,16,128]{2,1,0:T(8,128)}), f32[8,16,128]{2,1,0:T(8,128)S(1)}, u32[]{:S(2)}, u32[]{:S(2)}) async-start(f32[8,16,128]{2,1,0:T(8,128)} %bitcast.1), calls=%async_computation | async-start | bytes 131072 | tf_op jit(solution)/shard_map/all_to_all | solution.py:357
  12.6 3.0 %copy-start.4 = (f32[1,2,1,16,2,2048]{5,4,3,2,1,0:T(2,128)S(1)}, f32[1,2,1,16,2,2048]{5,4,3,2,1,0:T(2,128)}, u32[]{:S(2)}) copy-start(f32[1,2,1,16,2,2048]{5,4,3,2,1,0:T(2,128)} %param.6) | copy-start | bytes 1572868
  12.6 3.5 %copy-start.3 = (s32[1,2,2048]{2,1,0:T(2,128)S(1)}, s32[1,2,2048]{2,1,0:T(2,128)}, u32[]{:S(2)}) copy-start(s32[1,2,2048]{2,1,0:T(2,128)} %param.9) | copy-start | bytes 49156
  12.7 3.7 %copy-start.2 = (f32[1,2,8,1,16,64]{5,4,3,2,1,0:T(8,128)S(1)}, f32[1,2,8,1,16,64]{5,4,3,2,1,0:T(8,128)}, u32[]{:S(2)}) copy-start(f32[1,2,8,1,16,64]{5,4,3,2,1,0:T(8,128)} %param.11) | copy-start | bytes 196612
  18.7 22.7 %all-to-all-start.1 = ((f32[16,3,4,128]{3,2,1,0:T(4,128)}), f32[16,3,4,128]{3,2,1,0:T(4,128)S(1)}, u32[]{:S(2)}, u32[]{:S(2)}) async-start(f32[16,3,4,128]{3,2,1,0:T(4,128)} %bitcast.11), calls=%async_computation.1 | async-start | bytes 196608 | tf_op jit(solution)/shard_map/all_to_all | solution.py:357
  69.5 16.1 %all-to-all-start.4 = ((f32[4,3,4,128]{3,2,1,0:T(4,128)}), f32[4,3,4,128]{3,2,1,0:T(4,128)S(1)}, u32[]{:S(2)}, u32[]{:S(2)}) async-start(f32[4,3,4,128]{3,2,1,0:T(4,128)} %bitcast.17), calls=%async_computation.4 | async-start | bytes 49152 | tf_op jit(solution)/shard_map/all_to_all | solution.py:357
  122.9 20.0 %all-to-all-start.7 = ((f32[32,4,128]{2,1,0:T(4,128)}), f32[32,4,128]{2,1,0:T(4,128)S(1)}, u32[]{:S(2)}, u32[]{:S(2)}) async-start(f32[32,4,128]{2,1,0:T(4,128)} %bitcast.25), calls=%async_computation.7 | async-start | bytes 131072 | tf_op jit(solution)/shard_map/all_to_all | solution.py:357
  129.3 8.5 %collective-permute-start = (f32[128,128]{1,0:T(8,128)S(1)}, f32[128,128]{1,0:T(8,128)S(1)}, u32[]{:S(2)}, u32[]{:S(2)}) collective-permute-start(f32[128,128]{1,0:T(8,128)S(1)} %get-tuple-element.39.own), channel_id=1, source_target_pairs={{0,128},{128,256},{256,384},{384,0},{1,129},{129,257},{257,385},{3... | collective-permute-start | bytes 196616 | tf_op jit(solution)/shard_map/ppermute | solution.py:354
  131.3 6.8 %collective-permute-start.1 = (f32[128,128]{1,0:T(8,128)S(1)}, f32[128,128]{1,0:T(8,128)S(1)}, u32[]{:S(2)}, u32[]{:S(2)}) collective-permute-start(f32[128,128]{1,0:T(8,128)S(1)} %get-tuple-element.39.own), channel_id=1, source_target_pairs={{0,256},{128,384},{256,0},{384,128},{1,257},{129,385},{257,1},{385... | collective-permute-start | bytes 196616 | tf_op jit(solution)/shard_map/ppermute | solution.py:354
  134.9 5.1 %collective-permute-start.2 = (f32[128,128]{1,0:T(8,128)S(1)}, f32[128,128]{1,0:T(8,128)S(1)}, u32[]{:S(2)}, u32[]{:S(2)}) collective-permute-start(f32[128,128]{1,0:T(8,128)S(1)} %get-tuple-element.39.own), channel_id=1, source_target_pairs={{0,384},{128,0},{256,128},{384,256},{1,385},{129,1},{257,129},{385... | collective-permute-start | bytes 196616 | tf_op jit(solution)/shard_map/ppermute | solution.py:354

commit v2 on v0

--- a/solution.py
+++ b/solution.py
@@ -12,7 +12,7 @@
 RHO = 128.0
 F32, BF16 = jnp.float32, jnp.bfloat16
 NT = (((1,), (1,)), ((), ()))
-BC = 512
+BC = 1024
 VM = pl.BlockSpec(memory_space=pltpu.VMEM)
 SD = jax.ShapeDtypeStruct
 CUBE = ("y", "c", "zl")
@@ -313,7 +313,7 @@
             for t in range(2):
                 for r in range(2): out[r,t,:,D]=res[t][r]
         return 0
-    lax.fori_loop(0,BL//BC,chunk,0,unroll=4)
+    lax.fori_loop(0,BL//BC,chunk,0,unroll=2)
 
 
 def kernel(body, outs, ins, scratch=(), flops=100000000, vmem=8, moved=1000000):
@@ -342,8 +342,8 @@
     pairs = SD((256, 128), F32)
     moments = SD((192, 128), F32)
 
-    def other(j, s):
-        return lax.ppermute(j, "x", [(i, (i + s) % CL) for i in range(CL)])
+    def others(j):
+        return [lax.ppermute(j, "x", [(i, (i + s) % CL) for i in range(CL)]) for s in range(1, CL)]
 
     def swap(x, axes, *shape):
         return exchange(x.reshape(*shape, 128), axes).reshape(-1, 128)
@@ -369,14 +369,12 @@
     got = swap(send, CUBE, 32, 5, 2)
     part, j2 = kernel(second_update_kernel, (moments, full), 3, [tile])(got, zh, ab)
     got = swap(part, ("x", "zh"), 16, 3, 4)
-    r2, r3 = other(j2, 2), other(j2, 3)
+    d2 = others(j2)
     cnt2 = kernel(gate_kernel, SD((8, 128), F32), 1)(cnt)
+    rows, res = kernel(residual_kernel, (SD((256, ST), F32), SD((2, 2, SI, BL), F32)), 9, spread, big, 24)(
+        j2, *d2, tmap, cnt2, ants, m, v)
     z = kernel(last_fit_kernel, full, 3)(got, tmap, cnt)
-    z = swap(z, CUBE, 32, 4)
-    r1 = other(j2, 1)
-    rows, res = kernel(residual_kernel, (SD((256, ST), F32), SD((2, 2, SI, BL), F32)), 9, spread, big, 24)(
-        j2, r1, r2, r3, tmap, cnt2, ants, m, v)
-    zrows = kernel(unpack_kernel, SD((256, ST), F32), 1)(z)
+    zrows = kernel(unpack_kernel, SD((256, ST), F32), 1)(swap(z, CUBE, 32, 4))
     shape = gains_init.shape
     return rows.reshape(shape), zrows.reshape(shape), res.transpose(0, 2, 1, 3)[None, :, None]
 

time: 144 us -> 144 us (level)
  no operation moved by 1% of the time
where the time goes in v2:
time: 144 us; the launch traced here: 142 us
  blocking collectives  61.8 us (43%)
  starting transfers between devices  40.3 us (28%)
  Pallas kernels  18 us (12%)
  waiting for transfers between devices  15.4 us (11%)
  other arithmetic  3.51 us (2%)
  local copies, waits for them, and re-layouts  2.28 us (2%)
    all_to_all x3, blocking collectives, swap(): return exchange(x.reshape(*shape, 128), axes).reshape(-1, 128)  52.2 us
    all_to_all x4, starting transfers between devices, swap(): return exchange(x.reshape(*shape, 128), axes).reshape(-1, 128)  31.9 us
    all_to_all x4, waiting for transfers between devices, swap(): return exchange(x.reshape(*shape, 128), axes).reshape(-1, 128)  13.2 us
    all_to_all x1, blocking collectives, on_device(): exchange(kernel(update_kernel, SD((576, 128), F32), 3, [tile, tile])(got,...  9.6 us
    ppermute x3, starting transfers between devices, others(): lax.ppermute(j, 'x', [(i, (i + s) % CL) for i in range(CL)])  8.41 us
    pallas_call x1, Pallas kernels, on_device(): kernel(second_kernel, pairs, 6, scratch, big, 24)  5.58 us
    pallas_call x1, Pallas kernels, on_device(): ab = kernel(first_kernel, pairs, 4, scratch, big, 24)(gains, ants, m, v)  5.36 us
    transpose x1, other arithmetic, on_device(): jnp.where(keep[None, None], model[0][:, :, 0], jnp.zeros((), BF16))  3.01 us
  transfers between devices with their start and end apart: 7, of which 5 were waited for; matrix products, arithmetic and copies ran while one was open for 3% of the time, Pallas kernels for 9%

profile of v2, /device:TPU:1, one launch (start us, length us, event | category | flops | bytes accessed | tf_op | source)
XLA Modules:
  0.0 142.1 jit_solution(3901470067732867810)
XLA Ops:
  0.6 0.0 copy-start
  0.6 0.0 copy-start.1
  0.7 0.9 copy-done.1
  1.6 0.7 shard_map.85
  2.3 10.1 %all-to-all-start = ((f32[8,16,128]{2,1,0:T(8,128)}), f32[8,16,128]{2,1,0:T(8,128)S(1)}, u32[]{:S(2)}, u32[]{:S(2)}) async-start(f32[8,16,128]{2,1,0:T(8,128)} %bitcast.1), calls=%async_computation | async-start | bytes 131072 | tf_op jit(solution)/shard_map/all_to_all | solution.py:349
  12.4 0.0 copy-done
  12.4 0.0 copy-done.5
  12.4 0.2 compare_bitcast_fusion
  12.6 0.1 copy.9
  12.6 0.0 copy-start.4
  12.6 0.0 copy-start.3
  12.7 0.0 copy-start.2
  12.7 3.0 %fusion.m_ref = bf16[2,2,8,16,2048]{4,3,2,1,0:T(8,128)(2,1)S(1)} fusion(bf16[1,2,8,1,16,2,2048]{6,5,4,3,2,1,0:T(2,128)(2,1)} %param.7, pred[16,2,2048]{2,0,1:T(8,128)(4,1)S(1)} %copy.9), kind=kLoop, calls=%fused_computation.1 | loop fusion | flops 1048576 | bytes 4259840 | tf_op jit(solution)/shard_map/transpose | solution.py:353
  15.7 0.0 copy-done.4
  15.7 0.3 fusion.1.v_ref
  16.1 0.1 broadcast_in_dim.52.own
  16.1 0.0 copy-done.3
  16.1 0.3 shard_map.86
  16.4 0.8 all-to-all-done
  17.2 0.8 shard_map.87
  18.1 10.8 %all-to-all-start.1 = ((f32[16,3,4,128]{3,2,1,0:T(4,128)}), f32[16,3,4,128]{3,2,1,0:T(4,128)S(1)}, u32[]{:S(2)}, u32[]{:S(2)}) async-start(f32[16,3,4,128]{3,2,1,0:T(4,128)} %bitcast.11), calls=%async_computation.1 | async-start | bytes 196608 | tf_op jit(solution)/shard_map/all_to_all | solution.py:349
  28.8 0.0 copy-done.2
  28.8 5.4 %shard_map.88.ab = f32[256,128]{1,0:T(8,128)S(1)} custom-call(f32[256,64]{1,0:T(8,128)S(1)} %bitcast.60, s32[2,2048]{1,0:T(2,128)S(1)} %get-tuple-element.26.ants, bf16[2,2,8,16,2048]{4,3,2,1,0:T(8,128)(2,1)S(1)} %fusion.m_ref, f32[2,2,16,2048]{3,2,1,0:T(8,128)S(1)} %fusion.1.v_ref), custom_call_target="tpu_custom_call" | custom-call | flops 2000000000 | bytes 1000000 | tf_op jit(solution)/shard_map/pallas_call | solution.py:359
  34.2 6.5 %all-to-all-done.1 = f32[16,3,4,128]{3,2,1,0:T(4,128)S(1)} async-done(((f32[16,3,4,128]{3,2,1,0:T(4,128)}), f32[16,3,4,128]{3,2,1,0:T(4,128)S(1)}, u32[]{:S(2)}, u32[]{:S(2)}) %all-to-all-start.1) | async-done | bytes 98336 | tf_op jit(solution)/shard_map/all_to_all | solution.py:349
  40.7 0.2 shard_map.89
  40.9 16.4 %all_to_all.46 = f32[32,5,2,128]{3,2,1,0:T(2,128)S(1)} all-to-all(f32[32,5,2,128]{3,2,1,0:T(2,128)S(1)} %bitcast.50), channel_id=1, replica_groups=mesh['x'=4,'y'=4,'zh'=4,'zl'=4,'c'=2] {'y','c','zl'}, dimensions={0} | all-to-all | bytes 327680 | tf_op jit(solution)/shard_map/all_to_all | solution.py:349
  57.3 0.2 shard_map.90
  57.5 9.6 %all_to_all.47 = f32[4,144,128]{2,1,0:T(8,128)S(1)} all-to-all(f32[4,144,128]{2,1,0:T(8,128)S(1)} %bitcast.46), channel_id=1, replica_groups=mesh['x'=4,'y'=4,'zh'=4,'zl'=4,'c'=2] {'x'}, dimensions={0} | all-to-all | bytes 589824 | tf_op jit(solution)/shard_map/all_to_all | solution.py:364
  67.1 0.8 shard_map.91
  67.9 4.6 %all-to-all-start.4 = ((f32[4,3,4,128]{3,2,1,0:T(4,128)}), f32[4,3,4,128]{3,2,1,0:T(4,128)S(1)}, u32[]{:S(2)}, u32[]{:S(2)}) async-start(f32[4,3,4,128]{3,2,1,0:T(4,128)} %bitcast.17), calls=%async_computation.4 | async-start | bytes 49152 | tf_op jit(solution)/shard_map/all_to_all | solution.py:349
  72.6 5.6 %shard_map.92.ab = f32[256,128]{1,0:T(8,128)S(1)} custom-call(f32[576,128]{1,0:T(8,128)S(1)} %bitcast.45, bf16[512,128]{1,0:T(8,128)(2,1)S(1)} %get-tuple-element.33.t_ref, f32[8,128]{1,0:T(8,128)S(1)} %get-tuple-element.34.cnt.x_ref, s32[2,2048]{1,0:T(2,128)S(1)} %get-tuple-element.26.ants, bf16[2,2,8,16,2048]{4,3,2,1,0:T(8,128)(2,1)S(1)} %fusion.m_ref, ...), custom_call_target="tpu_custom_call" | custom-call | flops 2000000000 | bytes 1000000 | tf_op jit(solution)/shard_map/pallas_call | solution.py:367
  78.2 5.9 %all-to-all-done.4 = f32[4,3,4,128]{3,2,1,0:T(4,128)S(1)} async-done(((f32[4,3,4,128]{3,2,1,0:T(4,128)}), f32[4,3,4,128]{3,2,1,0:T(4,128)S(1)}, u32[]{:S(2)}, u32[]{:S(2)}) %all-to-all-start.4) | async-done | bytes 24608 | tf_op jit(solution)/shard_map/all_to_all | solution.py:349
  84.1 0.2 shard_map.93
  84.3 16.0 %all_to_all.48 = f32[32,5,2,128]{3,2,1,0:T(2,128)S(1)} all-to-all(f32[32,5,2,128]{3,2,1,0:T(2,128)S(1)} %bitcast.51), channel_id=1, replica_groups=mesh['x'=4,'y'=4,'zh'=4,'zl'=4,'c'=2] {'y','c','zl'}, dimensions={0} | all-to-all | bytes 327680 | tf_op jit(solution)/shard_map/all_to_all | solution.py:349
  100.3 0.2 shard_map.94
  100.5 19.8 %all_to_all.49 = f32[16,3,4,128]{3,2,1,0:T(4,128)S(1)} all-to-all(f32[16,3,4,128]{3,2,1,0:T(4,128)S(1)} %bitcast.53), channel_id=1, replica_groups=mesh['x'=4,'y'=4,'zh'=4,'zl'=4,'c'=2] {'x','zh'}, dimensions={0} | all-to-all | bytes 196608 | tf_op jit(solution)/shard_map/all_to_all | solution.py:349
  120.3 1.0 shard_map.97
  121.2 6.4 %all-to-all-start.7 = ((f32[32,4,128]{2,1,0:T(4,128)}), f32[32,4,128]{2,1,0:T(4,128)S(1)}, u32[]{:S(2)}, u32[]{:S(2)}) async-start(f32[32,4,128]{2,1,0:T(4,128)} %bitcast.25), calls=%async_computation.7 | async-start | bytes 131072 | tf_op jit(solution)/shard_map/all_to_all | solution.py:349
  127.6 1.9 %collective-permute-start = (f32[128,128]{1,0:T(8,128)S(1)}, f32[128,128]{1,0:T(8,128)S(1)}, u32[]{:S(2)}, u32[]{:S(2)}) collective-permute-start(f32[128,128]{1,0:T(8,128)S(1)} %get-tuple-element.37.own), channel_id=1, source_target_pairs={{0,128},{128,256},{256,384},{384,0},{1,129},{129,257},{257,385},{3... | collective-permute-start | bytes 196616 | tf_op jit(solution)/shard_map/ppermute | solution.py:346
  129.6 3.7 %collective-permute-start.1 = (f32[128,128]{1,0:T(8,128)S(1)}, f32[128,128]{1,0:T(8,128)S(1)}, u32[]{:S(2)}, u32[]{:S(2)}) collective-permute-start(f32[128,128]{1,0:T(8,128)S(1)} %get-tuple-element.37.own), channel_id=1, source_target_pairs={{0,256},{128,384},{256,0},{384,128},{1,257},{129,385},{257,1},{385... | collective-permute-start | bytes 196616 | tf_op jit(solution)/shard_map/ppermute | solution.py:346
  133.2 2.8 %collective-permute-start.2 = (f32[128,128]{1,0:T(8,128)S(1)}, f32[128,128]{1,0:T(8,128)S(1)}, u32[]{:S(2)}, u32[]{:S(2)}) collective-permute-start(f32[128,128]{1,0:T(8,128)S(1)} %get-tuple-element.37.own), channel_id=1, source_target_pairs={{0,384},{128,0},{256,128},{384,256},{1,385},{129,1},{257,129},{385... | collective-permute-start | bytes 196616 | tf_op jit(solution)/shard_map/ppermute | solution.py:346
  136.1 0.0 collective-permute-done.r1
  136.1 0.3 collective-permute-done.1.r2
  136.4 1.9 %collective-permute-done.2.r3 = f32[128,128]{1,0:T(8,128)S(1)} collective-permute-done((f32[128,128]{1,0:T(8,128)S(1)}, f32[128,128]{1,0:T(8,128)S(1)}, u32[]{:S(2)}, u32[]{:S(2)}) %collective-permute-start.2) | collective-permute-done | bytes 65568 | tf_op jit(solution)/shard_map/ppermute | solution.py:346
  138.3 1.8 %shard_map.96 = (f32[256,64]{1,0:T(8,128)}, f32[2,2,16,2048]{3,2,1,0:T(8,128)S(1)}) custom-call(f32[128,128]{1,0:T(8,128)S(1)} %get-tuple-element.37.own, f32[128,128]{1,0:T(8,128)S(1)} %collective-permute-done.r1, f32[128,128]{1,0:T(8,128)S(1)} %collective-permute-done.1.r2, f32[128,128]{1,0:T(8,128)S(1)} %collective-permute-done.2.r3, ...), custom_call_target="tpu_custom_call" | custom-call | flops 2000000000 | bytes 1000000 | tf_op jit(solution)/shard_map/pallas_call | solution.py:374
  140.1 1.2 copy.15
  141.3 0.0 all-to-all-done.7
  141.3 0.7 shard_map.98
  (5 shorter events, 0.0 us)
Async XLA Ops:
  0.6 11.7 %copy-start = (s32[4,4,40]{2,1,0:T(4,128)S(1)}, s32[4,4,40]{2,1,0:T(4,128)}, u32[]{:S(2)}) copy-start(s32[4,4,40]{2,1,0:T(4,128)} %param.10) | copy-start | bytes 7684
  0.6 0.9 copy-start.1
  1.6 10.8 %copy-start.5 = (s32[1,1,16,2,2048]{4,3,2,1,0:T(2,128)S(1)}, s32[1,1,16,2,2048]{4,3,2,1,0:T(2,128)}, u32[]{:S(2)}) copy-start(s32[1,1,16,2,2048]{4,3,2,1,0:T(2,128)} %param.8) | copy-start | bytes 786436
  2.3 15.0 %all-to-all-start = ((f32[8,16,128]{2,1,0:T(8,128)}), f32[8,16,128]{2,1,0:T(8,128)S(1)}, u32[]{:S(2)}, u32[]{:S(2)}) async-start(f32[8,16,128]{2,1,0:T(8,128)} %bitcast.1), calls=%async_computation | async-start | bytes 131072 | tf_op jit(solution)/shard_map/all_to_all | solution.py:349
  12.6 3.0 %copy-start.4 = (f32[1,2,1,16,2,2048]{5,4,3,2,1,0:T(2,128)S(1)}, f32[1,2,1,16,2,2048]{5,4,3,2,1,0:T(2,128)}, u32[]{:S(2)}) copy-start(f32[1,2,1,16,2,2048]{5,4,3,2,1,0:T(2,128)} %param.6) | copy-start | bytes 1572868
  12.6 3.5 %copy-start.3 = (s32[1,2,2048]{2,1,0:T(2,128)S(1)}, s32[1,2,2048]{2,1,0:T(2,128)}, u32[]{:S(2)}) copy-start(s32[1,2,2048]{2,1,0:T(2,128)} %param.9) | copy-start | bytes 49156
  12.7 16.2 %copy-start.2 = (f32[1,2,8,1,16,64]{5,4,3,2,1,0:T(8,128)S(1)}, f32[1,2,8,1,16,64]{5,4,3,2,1,0:T(8,128)}, u32[]{:S(2)}) copy-start(f32[1,2,8,1,16,64]{5,4,3,2,1,0:T(8,128)} %param.11) | copy-start | bytes 196612
  18.1 22.6 %all-to-all-start.1 = ((f32[16,3,4,128]{3,2,1,0:T(4,128)}), f32[16,3,4,128]{3,2,1,0:T(4,128)S(1)}, u32[]{:S(2)}, u32[]{:S(2)}) async-start(f32[16,3,4,128]{3,2,1,0:T(4,128)} %bitcast.11), calls=%async_computation.1 | async-start | bytes 196608 | tf_op jit(solution)/shard_map/all_to_all | solution.py:349
  67.9 16.1 %all-to-all-start.4 = ((f32[4,3,4,128]{3,2,1,0:T(4,128)}), f32[4,3,4,128]{3,2,1,0:T(4,128)S(1)}, u32[]{:S(2)}, u32[]{:S(2)}) async-start(f32[4,3,4,128]{3,2,1,0:T(4,128)} %bitcast.17), calls=%async_computation.4 | async-start | bytes 49152 | tf_op jit(solution)/shard_map/all_to_all | solution.py:349
  121.2 20.1 %all-to-all-start.7 = ((f32[32,4,128]{2,1,0:T(4,128)}), f32[32,4,128]{2,1,0:T(4,128)S(1)}, u32[]{:S(2)}, u32[]{:S(2)}) async-start(f32[32,4,128]{2,1,0:T(4,128)} %bitcast.25), calls=%async_computation.7 | async-start | bytes 131072 | tf_op jit(solution)/shard_map/all_to_all | solution.py:349
  127.6 8.5 %collective-permute-start = (f32[128,128]{1,0:T(8,128)S(1)}, f32[128,128]{1,0:T(8,128)S(1)}, u32[]{:S(2)}, u32[]{:S(2)}) collective-permute-start(f32[128,128]{1,0:T(8,128)S(1)} %get-tuple-element.37.own), channel_id=1, source_target_pairs={{0,128},{128,256},{256,384},{384,0},{1,129},{129,257},{257,385},{3... | collective-permute-start | bytes 196616 | tf_op jit(solution)/shard_map/ppermute | solution.py:346
  129.6 6.8 %collective-permute-start.1 = (f32[128,128]{1,0:T(8,128)S(1)}, f32[128,128]{1,0:T(8,128)S(1)}, u32[]{:S(2)}, u32[]{:S(2)}) collective-permute-start(f32[128,128]{1,0:T(8,128)S(1)} %get-tuple-element.37.own), channel_id=1, source_target_pairs={{0,256},{128,384},{256,0},{384,128},{1,257},{129,385},{257,1},{385... | collective-permute-start | bytes 196616 | tf_op jit(solution)/shard_map/ppermute | solution.py:346
  133.2 5.1 %collective-permute-start.2 = (f32[128,128]{1,0:T(8,128)S(1)}, f32[128,128]{1,0:T(8,128)S(1)}, u32[]{:S(2)}, u32[]{:S(2)}) collective-permute-start(f32[128,128]{1,0:T(8,128)S(1)} %get-tuple-element.37.own), channel_id=1, source_target_pairs={{0,384},{128,0},{256,128},{384,256},{1,385},{129,1},{257,129},{385... | collective-permute-start | bytes 196616 | tf_op jit(solution)/shard_map/ppermute | solution.py:346
